TPU v7x, 32 devices: a 4x4x1 block of a 4x4x8 slice. The times are simulated.
32 devices in a mesh: dp: 2 (over z, core), sp: 16 (over x, y).
Axes of the slice: x: 4, y: 4, z: 1, core: 2. Of those that a mesh axis runs over, the one named last changes fastest.
The devices are a block of a 4x4x8 slice.
Arguments:
- q: bfloat16 [64, 56, 128], P('dp'), parts along dimension 0
- k: bfloat16 [64, 2048, 56, 128], P('dp', 'sp'), parts along dimension 0
- v: bfloat16 [64, 2048, 56, 128], P('dp', 'sp'), parts along dimension 0
Outputs:
- q: bfloat16 [64, 56, 128], P('dp'), parts along dimension 0
There are 2 independent parts. A program takes and returns all parts, laid end to end along the dimension named above; each array names one.
All inputs are finite; a program needn't handle non-finite values.
Results may differ from a plain program's by a relative error of at most 0.012.
Values are sent between devices in bfloat16 or wider.
A program may use at most 768 MiB of HBM per device.

v0:
```python
import jax
import jax.numpy as jnp
from jax import lax
from jax.sharding import PartitionSpec as P


def einsum(form, a, b):
    return jnp.einsum(form, a.astype(jnp.float32), b.astype(jnp.float32))


def part_of(q, k, v):
    grouped = q.reshape(q.shape[0], k.shape[2], -1, q.shape[2])
    scores = einsum("bgsd,bugd->bgsu", grouped, k) * q.shape[2] ** -0.5
    high = jnp.max(scores, -1, keepdims=True)
    weights = jnp.exp(scores - high)
    seen = einsum("bgsu,bugd->bgsd", weights.astype(jnp.bfloat16), v)
    return jnp.concatenate([seen, jnp.sum(weights, -1, keepdims=True), high], -1)


def together(parts):
    seen, total, high = parts[..., :-2], parts[..., -2:-1], parts[..., -1:]
    scale = jnp.exp(high - jnp.max(high, 0))
    return (jnp.sum(seen * scale, 0) / jnp.sum(total * scale, 0)).astype(jnp.bfloat16)


def solution(mesh):
    def step(q, k, v):
        return together(lax.all_gather(part_of(q, k, v), "sp")).reshape(q.shape)

    return jax.shard_map(
        step,
        mesh=mesh,
        in_specs=(P("dp", None, None), P("dp", "sp", None, None), P("dp", "sp", None, None)),
        out_specs=P("dp", None, None),
        check_vma=False,
    )
```

profile of v0, /device:TPU:97, one launch (start us, length us, event | category | flops | bytes accessed | tf_op | source)
XLA Modules:
  0.0 294.7 jit_solution(13967744038691786033)
XLA Ops:
  6.5 0.0 all-gather.3.cloned.1.call-start
  6.6 38.3 %fusion.2 = f32[32,56,1,128]{3,2,1,0:T(1,128)S(1)} fusion(bf16[32,128,56,128]{3,2,1,0:T(8,128)(2,1)} %param.4, bf16[32,56,128,1]{2,1,0,3:T(8,128)(2,1)} %bitcast.18), kind=kOutput, calls=%fused_computation.2 | convolution fusion | flops 58720256 | bytes 60096512 | tf_op jit(solution)/shard_map/bgsd,bugd->bgsu/dot_general | solution.py:8
  44.9 0.3 multiply_reduce_fusion
  45.2 0.6 fusion.9
  45.8 22.6 %fusion = f32[32,56,1,128]{3,2,1,0:T(1,128)S(1)} fusion(bf16[32,128,56,128]{3,2,1,0:T(8,128)(2,1)} %param.5, bf16[32,56,128,1]{2,1,0,3:T(8,128)(2,1)S(1)} %get-tuple-element.7), kind=kOutput, calls=%fused_computation | convolution fusion | flops 58720256 | bytes 60096512 | tf_op jit(solution)/shard_map/bgsu,bugd->bgsd/dot_general | solution.py:8
  68.4 1.2 copy.12
  69.6 1.6 pad_maximum_fusion
  71.2 0.1 all-gather.3.cloned.1.call-update
  71.2 198.3 %all-gather.3.cloned.1.call-done = f32[512,56,1,130]{1,0,3,2:T(8,128)} async-done(((f32[32,56,1,130]{1,0,3,2:T(8,128)}), f32[512,56,1,130]{1,0,3,2:T(8,128)}) %all-gather.3.cloned.1.call-update) | async-done | bytes 14909456 | tf_op jit(solution)/shard_map/all_gather | solution.py:28
  269.5 1.0 slice_reduce_fusion
  270.5 1.1 fusion.10
  271.6 14.1 %fusion.4 = f32[32,56,128]{1,0,2:T(8,128)S(1)} fusion(f32[16,32,56,1,130]{2,1,0,4,3:T(8,128)} %bitcast.13, f32[16,32,56]{2,1,0:T(8,128)S(1)} %get-tuple-element.6), kind=kLoop, calls=%fused_computation.5 | loop fusion | flops 7110656 | bytes 15712256 | tf_op jit(solution)/shard_map/reduce_sum | solution.py:23
  285.7 0.2 divide_convert_fusion
  286.0 1.8 copy.6
Async XLA Ops:
  6.5 263.0 %all-gather.3.cloned.1.call-start = ((), (), s32[]{:S(2)}) async-start(), calls=%async_computation | async-start | bytes 36208640 | tf_op jit(solution)/shard_map/all_gather | solution.py:28
Sparse Core Ops, SparseCore 0:
  71.3 198.1 all-gather.2
where the time goes:
time: 295 us
  waiting for transfers between devices  198 us (67%)
  matrix products  60.9 us (21%)
  other arithmetic  18.9 us (6%)
  between operations  13.4 us (5%)
  local copies, waits for them, and re-layouts  3.03 us (1%)
    all_gather x1, waiting for transfers between devices, step(): return together(lax.all_gather(part_of(q, k, v), 'sp')).reshape(q.shape)  198 us
    dot_general x2, matrix products, einsum(): return jnp.einsum(form, a.astype(jnp.float32), b.astype(jnp.float32))  60.9 us
    reduce_sum x1, other arithmetic, together(): jnp.sum(seen * scale, 0) / jnp.sum(total * scale, 0)  14.1 us
  transfers between devices with their start and end apart: 1, of which 1 were waited for; matrix products, arithmetic and copies ran while one was open for 0% of the time, Pallas kernels for 0%

commit v1 on v0

v1 whole, which is shorter than its diff:
```python
import functools
import math

import jax
import jax.numpy as jnp
from jax import lax
from jax.experimental import pallas as pl
from jax.experimental.pallas import tpu as pltpu
from jax.sharding import PartitionSpec as P

MESH = pl.DeviceIdType.MESH
ROWS = 16
SLOTS = 6
LAG = 4


def attend(q2, keys, values, scale):
    twice, head = q2.shape
    lane = lax.broadcasted_iota(jnp.int32, (ROWS, 128), 1)
    row = lax.broadcasted_iota(jnp.int32, (ROWS, 128), 0)
    other = jnp.where(lane % ROWS == row, 0.0, -jnp.inf).astype(jnp.float32)
    seen, high, total = [], [], []
    for j in range(twice // ROWS):
        q = q2[j * ROWS : (j + 1) * ROWS]
        zero = jnp.zeros_like(q)
        both = jnp.concatenate([jnp.concatenate([q, zero], 1), jnp.concatenate([zero, q], 1)], 0)
        k = keys(j)
        half = k.shape[0] // 2
        k = jnp.concatenate([k[:half], k[half:]], 1)
        s = lax.dot_general(both, k, (((1,), (1,)), ((), ())), preferred_element_type=jnp.float32)
        pieces = [s[r : r + ROWS, c : c + 128] + other for r in (0, ROWS) for c in range(0, half, 128)]
        m = jnp.max(functools.reduce(jnp.maximum, pieces), -1, keepdims=True)
        w = [jnp.exp2((x - m) * scale) for x in pieces]
        total.append(jnp.sum(functools.reduce(jnp.add, w), -1, keepdims=True))
        n = half // 128
        w = jnp.concatenate([jnp.concatenate(w[:n], 1), jnp.concatenate(w[n:], 1)], 0).astype(jnp.bfloat16)
        v = values(j)
        v = jnp.concatenate([v[:half], v[half:]], 1)
        o = jnp.dot(w, v, preferred_element_type=jnp.float32)
        seen.append(o[:ROWS, :head] + o[ROWS:, head:])
        high.append(m)
    seen, high, total = (jnp.concatenate(x, 0) for x in (seen, high, total))
    heads = twice // 2
    m = jnp.maximum(high[:heads], high[heads:])
    a, b = jnp.exp2((high[:heads] - m) * scale), jnp.exp2((high[heads:] - m) * scale)
    return seen[:heads] * a + seen[heads:] * b, m, total[:heads] * a + total[heads:] * b


def kernel(side, scale, q_hbm, k_hbm, v_hbm, o_hbm, q2, kbuf, vbuf, ax, sx, ay, sy, out, ksem, vsem, qsem, osem, asend, ssend, xa, xs, ya, ys):
    n, heads, head = q_hbm.shape
    slots = kbuf.shape[0]
    me = lax.axis_index("sp")
    across, along = me // side, me % side

    def load(b):
        slot = b % slots
        return (
            pltpu.make_async_copy(k_hbm.at[b], kbuf.at[slot], ksem.at[slot]),
            pltpu.make_async_copy(v_hbm.at[b], vbuf.at[slot], vsem.at[slot]),
        )

    queries = [pltpu.make_async_copy(q_hbm, q2.at[:, pl.ds(i * heads, heads)], qsem.at[i]) for i in range(2)]
    for copy in queries:
        copy.start()
    for b in range(slots):
        for copy in load(b):
            copy.start()

    def to_x(d):
        return across * side + (along + d) % side

    def to_y(d):
        return ((across + d) % side) * side + along

    barrier = pltpu.get_barrier_semaphore()
    for d in range(1, side):
        for to in (to_x, to_y):
            pl.semaphore_signal(barrier, inc=1, device_id={"sp": to(d)}, device_id_type=MESH)
    pl.semaphore_wait(barrier, 2 * (side - 1))

    def send(b, to, phase, acc, stat, acc_sem, stat_sem):
        for d in range(1, side):
            for buf, out_sem, in_sem in ((stat, ssend, stat_sem), (acc, asend, acc_sem)):
                pltpu.make_async_remote_copy(
                    src_ref=buf.at[b, 0],
                    dst_ref=buf.at[b, d],
                    send_sem=out_sem.at[phase],
                    recv_sem=in_sem.at[b],
                    device_id={"sp": to(d)},
                    device_id_type=MESH,
                ).start()

    def arrived(b, buf, sem):
        part = buf.at[b, pl.ds(1, side - 1)]
        pltpu.make_async_copy(part, part, sem.at[b]).wait()

    eye = lax.broadcasted_iota(jnp.int32, (heads, 128), 0) == lax.broadcasted_iota(jnp.int32, (heads, 128), 1)

    def to_row(column):
        return jnp.sum(jnp.where(eye, column, 0.0), 0, keepdims=True)

    def to_column(row):
        return jnp.sum(jnp.where(eye, row, 0.0), 1, keepdims=True)

    def merged(b, acc, stat, mine, last):
        slot = [(mine - c + side) % side for c in range(side)]
        high = [stat[b, s, 0:1, :] for s in slot]
        m = functools.reduce(jnp.maximum, high)
        w = [jnp.exp2((h - m) * scale) for h in high]
        total = functools.reduce(jnp.add, [x * stat[b, s, 1:2, :] for x, s in zip(w, slot)])
        if last:
            w = [x / total for x in w]
        seen = functools.reduce(jnp.add, [to_column(x) * acc[b, s].astype(jnp.float32) for x, s in zip(w, slot)])
        return seen.astype(jnp.bfloat16), m, total

    def own(b):
        for copy in load(b):
            copy.wait()

    def work(b):
        slot = b % slots
        rows = lambda buf: lambda j: buf[slot, :, j * ROWS : (j + 1) * ROWS, :].reshape(-1, head)
        seen, m, total = attend(q2[b], rows(kbuf), rows(vbuf), scale)
        ax[b, 0] = seen.astype(jnp.bfloat16)
        sx[b, 0, 0:1, :] = to_row(m)
        sx[b, 0, 1:2, :] = to_row(total)

    def wait_x(b):
        arrived(b, ax, xa)
        arrived(b, sx, xs)

    def wait_y(b):
        arrived(b, ay, ya)
        arrived(b, sy, ys)

    def x_merge(b):
        ay[b, 0], sy[b, 0, 0:1, :], sy[b, 0, 1:2, :] = merged(b, ax, sx, along, False)

    def y_merge(b):
        out[b] = merged(b, ay, sy, across, True)[0]

    def send_x(b):
        send(b, to_x, 0, ax, sx, xa, xs)

    def send_y(b):
        send(b, to_y, 1, ay, sy, ya, ys)

    def put(b):
        pltpu.make_async_copy(out.at[b], o_hbm.at[b], osem).start()

    def step(b, x, y, more):
        own(b)
        if x:
            wait_x(b - LAG)
        if y:
            wait_y(b - 2 * LAG)
        work(b)
        if x:
            x_merge(b - LAG)
        if y:
            y_merge(b - 2 * LAG)
        send_x(b)
        if x:
            send_y(b - LAG)
        if y:
            put(b - 2 * LAG)
        if more:
            for copy in load(b + slots):
                copy.start()

    for copy in queries:
        copy.wait()

    def loop(first, end, *kinds):
        @pl.loop(first, end)
        def _(b):
            step(b, *kinds)

    loop(0, LAG, False, False, True)
    loop(LAG, 2 * LAG, True, False, True)
    loop(2 * LAG, n - slots, True, True, True)
    loop(n - slots, n, True, True, False)

    @pl.loop(n - LAG, n)
    def _(b):
        wait_x(b)
        x_merge(b)
        send_y(b)
        wait_y(b - LAG)
        y_merge(b - LAG)
        put(b - LAG)

    @pl.loop(n - LAG, n)
    def _(b):
        wait_y(b)
        y_merge(b)
        put(b)

    pltpu.make_async_copy(out, o_hbm, osem).wait()
    for phase, (acc, stat) in enumerate(((ax, sx), (ay, sy))):
        for buf, sem in ((acc, asend), (stat, ssend)):
            part = buf.at[:, pl.ds(1, side - 1)]
            pltpu.make_async_copy(part, part, sem.at[phase]).wait()


def solution(mesh):
    side = math.isqrt(mesh.shape["sp"])

    def step(q, k, v):
        n, heads, head = q.shape
        tokens = k.shape[1]
        scale = head**-0.5 * math.log2(math.e)
        k, v = (x.reshape(n, tokens // 2, 2 * heads, head) for x in (k, v))
        any_ = pl.BlockSpec(memory_space=pl.ANY)
        dma = pltpu.SemaphoreType.DMA
        return pl.pallas_call(
            functools.partial(kernel, side, scale),
            out_shape=jax.ShapeDtypeStruct(q.shape, q.dtype),
            in_specs=[any_] * 3,
            out_specs=any_,
            scratch_shapes=[
                pltpu.VMEM((n, 2 * heads, head), q.dtype),
                pltpu.VMEM((SLOTS,) + k.shape[1:], k.dtype),
                pltpu.VMEM((SLOTS,) + v.shape[1:], v.dtype),
                pltpu.VMEM((n, side, heads, head), jnp.bfloat16),
                pltpu.VMEM((n, side, 2, 128), jnp.float32),
                pltpu.VMEM((n, side, heads, head), jnp.bfloat16),
                pltpu.VMEM((n, side, 2, 128), jnp.float32),
                pltpu.VMEM((n, heads, head), q.dtype),
                dma((SLOTS,)),
                dma((SLOTS,)),
                dma((2,)),
                dma,
                dma((2,)),
                dma((2,)),
                dma((n,)),
                dma((n,)),
                dma((n,)),
                dma((n,)),
            ],
            compiler_params=pltpu.CompilerParams(
                collective_id=0, has_side_effects=True, vmem_limit_bytes=56 * 2**20
            ),
            name="decode_attention",
        )(q, k, v)

    return jax.shard_map(
        step,
        mesh=mesh,
        in_specs=(P("dp", None, None), P("dp", "sp", None, None), P("dp", "sp", None, None)),
        out_specs=P("dp", None, None),
        check_vma=False,
    )
```

time: 295 us -> 107 us (0.36)
  waiting for transfers between devices: 198 us -> 0 us
  Pallas kernels: 0 us -> 105 us
  matrix products: 60.9 us -> 0 us
  other arithmetic: 18.9 us -> 0 us
  between operations: 13.4 us -> 0.01 us
    all_gather x1 -> x0, waiting for transfers between devices: 198 us -> none  [step(): return together(lax.all_gather(part_of(q, k, v), 'sp')).reshape(q.shape)]
    pallas_call x0 -> x1, Pallas kernels: none -> 105 us  [step(): pl.pallas_call(functools.partial(kernel, side, scale), out_shape=jax.Shap...]
    dot_general x2 -> x0, matrix products: 60.9 us -> none  [einsum(): return jnp.einsum(form, a.astype(jnp.float32), b.astype(jnp.float32))]
    reduce_sum x2 -> x0, other arithmetic: 15.2 us -> none  [the longest x1 14.1 us: together(): jnp.sum(seen * scale, 0) / jnp.sum(total * scale, 0)]
  transfers between devices with their start and end apart: 1 -> 0, of which waited for: 1 -> 0; matrix products, arithmetic and copies ran while one was open for 0% -> 0% of each run, Pallas kernels for 0% -> 0%
where the time goes in v1:
time: 107 us
  Pallas kernels  105 us (98%)
  local copies, waits for them, and re-layouts  1.82 us (2%)
    pallas_call x1, Pallas kernels, step(): pl.pallas_call(functools.partial(kernel, side, scale), out_shape=jax.Shap...  105 us

profile of v1, /device:TPU:97, one launch (start us, length us, event | category | flops | bytes accessed | tf_op | source)
XLA Modules:
  0.0 107.2 jit_solution(5888688426528704969)
XLA Ops:
  0.0 105.4 %decode_attention.1 = bf16[32,56,128]{2,1,0:T(8,128)(2,1)} custom-call(bf16[32,56,128]{2,1,0:T(8,128)(2,1)} %q_hbm.1, bf16[32,64,112,128]{3,2,1,0:T(8,128)(2,1)} %bitcast.2, bf16[32,64,112,128]{3,2,1,0:T(8,128)(2,1)} %bitcast.3), custom_call_target="tpu_custom_call" | custom-call | tf_op jit(solution)/shard_map/decode_attention/pallas_call | solution.py:216
  105.4 1.8 %copy.5 = bf16[32,56,128]{2,1,0:T(8,128)(2,1)} copy(bf16[32,56,128]{2,1,0:T(8,128)(2,1)} %decode_attention.1) | data formatting | bytes 917504

commit v2 on v0

v2 whole, which is shorter than its diff:
```python
import functools
import math

import jax
import jax.numpy as jnp
from jax import lax
from jax.experimental import pallas as pl
from jax.experimental.pallas import tpu as pltpu
from jax.sharding import PartitionSpec as P

MESH = pl.DeviceIdType.MESH
ROWS = 8
SLOTS = 6
PAIR = 2
LAG = 6
TILES = 2
WIDE = 256


def scores(q, tile):
    k = jnp.concatenate([tile(t) for t in range(TILES)], 0)
    return lax.dot_general(q, k, (((1,), (1,)), ((), ())), preferred_element_type=jnp.float32)


def weigh(s, scale):
    lane = lax.broadcasted_iota(jnp.int32, (ROWS, 128), 1)
    row = lax.broadcasted_iota(jnp.int32, (ROWS, 128), 0)
    other = jnp.where(lane % ROWS == row, 0.0, -jnp.inf).astype(jnp.float32)
    pieces = [[s[r : r + ROWS, c : c + 128] + other for c in range(0, s.shape[1], 128)] for r in (0, ROWS)]
    m = jnp.max(functools.reduce(jnp.maximum, [y for x in pieces for y in x]), -1, keepdims=True)
    m = jnp.broadcast_to(m, (ROWS, 128))
    w = [[jnp.exp2((y - m) * scale) for y in x] for x in pieces]
    total = jnp.sum(functools.reduce(jnp.add, [y for x in w for y in x]), -1, keepdims=True)
    total = jnp.broadcast_to(total, (ROWS, 128))
    return jnp.concatenate([jnp.concatenate(x, 1) for x in w], 0).astype(jnp.bfloat16), m, total


def values_seen(weights, tile):
    v = jnp.concatenate([tile(t) for t in range(TILES)], 0)
    return jnp.dot(weights, v, preferred_element_type=jnp.float32)


def order(keys, values):
    found, k, v, done_k, done_v = [], 0, 0, 0, 0
    last = min(values, 5)
    while k < keys or v < values:
        if k < keys:
            found.append(("k", k))
            k += 1
            if k == min(2, keys):
                found.append(("m", 0))
            if k - done_k > 3:
                found.append(("K", done_k))
                done_k += 1
            due = 0 if k < 3 else (values - last) * (k - 2) // max(keys - 2, 1)
        else:
            due = v + 1
        while v < due:
            found.append(("v", v))
            v += 1
            if v - done_v > 4:
                found.append(("V", done_v))
                done_v += 1
            if k == keys and done_k < keys:
                found.append(("K", done_k))
                done_k += 1
    found += [("K", j) for j in range(done_k, keys)] + [("V", j) for j in range(done_v, values)]
    return found if keys else [("m", 0)] + found


def kernel(
    side, scale, q_hbm, k_hbm, v_hbm, o_hbm, q2, kbuf, vbuf, wbuf, part, stat, out, racc, rstat, xacc, xstat, ypart, ysent, yacc,
    ystat, eacc, estat, ewide, ksem, vsem, qsem, osem, sent_acc, sent_stat, r_acc, r_stat, g_sent, g_in, x_acc, x_stat, y_acc,
    y_stat, e_acc, e_stat,
):
    n, classes, _, head = q_hbm.shape
    heads = classes * ROWS
    slots, _, tokens, _, _ = kbuf.shape
    me = lax.axis_index("sp")
    across, along = me // side, me % side

    def load(hbm, buf, sem, b):
        pltpu.make_async_copy(hbm.at[b], buf.at[b % slots], sem.at[b % slots]).start()

    def loaded(buf, sem, b):
        part = buf.at[b % slots]
        pltpu.make_async_copy(part, part, sem.at[b % slots]).wait()

    load_k, load_v = (functools.partial(load, *x) for x in ((k_hbm, kbuf, ksem), (v_hbm, vbuf, vsem)))
    wait_k, wait_v = (functools.partial(loaded, *x) for x in ((kbuf, ksem), (vbuf, vsem)))

    queries = [
        pltpu.make_async_copy(q_hbm, q2.at[:, :, pl.ds(i * ROWS, ROWS), pl.ds(i * head, head)], qsem.at[i])
        for i in range(2)
    ]
    for copy in queries:
        copy.start()
    for b in range(slots - 1):
        load_k(b)
        if b < slots - PAIR:
            load_v(b)
    zero = jnp.zeros((classes, ROWS, head), q2.dtype)

    @pl.loop(0, n)
    def _(b):
        q2[b, :, :ROWS, head:] = zero
        q2[b, :, ROWS:, :head] = zero

    group = side * side
    square = group + group // 2
    straight = n - 2

    def device(dx, dy):
        return ((across + dx) % side) * side + (along + dy) % side

    others = sorted(((dx, dy) for dx in range(side) for dy in range(side) if dx or dy), key=lambda d: -sum(min(x, side - x) for x in d))

    barrier = pltpu.get_barrier_semaphore()
    for dx, dy in others:
        pl.semaphore_signal(barrier, inc=1, device_id={"sp": device(dx, dy)}, device_id_type=MESH)
    pl.semaphore_wait(barrier, group - 1)

    def push(src, dst, to, send_sem, recv_sem):
        pltpu.make_async_remote_copy(
            src_ref=src, dst_ref=dst, send_sem=send_sem, recv_sem=recv_sem, device_id={"sp": to}, device_id_type=MESH
        ).start()

    def wait(like, sem):
        pltpu.make_async_copy(like, like, sem).wait()

    eye = lax.broadcasted_iota(jnp.int32, (heads, 128), 0) == lax.broadcasted_iota(jnp.int32, (heads, 128), 1)

    def to_row(column):
        return jnp.sum(jnp.where(eye, column, 0.0), 0, keepdims=True)

    def to_column(row):
        column = jnp.sum(jnp.where(eye, row, 0.0), 1, keepdims=True)
        return jnp.broadcast_to(column, (heads, 128))

    def shares(high, total, last):
        m = functools.reduce(jnp.maximum, high)
        w = [jnp.exp2((h - m) * scale) for h in high]
        total = functools.reduce(jnp.add, [x * t for x, t in zip(w, total)])
        return [x / total for x in w] if last else w, m, total

    def joined(accs, stats, last):
        w, m, total = shares([x[0:1, :] for x in stats], [x[1:2, :] for x in stats], last)
        seen = functools.reduce(jnp.add, [to_column(x) * acc.astype(jnp.float32) for x, acc in zip(w, accs)])
        return seen.astype(jnp.bfloat16), m, total

    def tile_of(buf, b, j):
        def tile(t):
            size = WIDE // ROWS
            rows = [buf[b % slots, p * size : (p + 1) * size, j].reshape(WIDE, head) for p in (2 * t, 2 * t + 1)]
            return jnp.concatenate(rows, 1)

        return tile

    def work(qk, pv, merge):
        started, made, seen = {}, {}, {}
        for kind, i in order(len(qk) * classes, len(pv) * classes):
            at, j = i // classes, i % classes
            if kind == "m":
                merge()
            elif kind == "k":
                b = qk[at]
                started[kind, i] = scores(q2[b, j], tile_of(kbuf, b, j))
            elif kind == "v":
                b = pv[at]
                started[kind, i] = values_seen(wbuf[b % (2 * PAIR), j], tile_of(vbuf, b, j))
            elif kind == "K":
                b = qk[at]
                w, m, total = weigh(started["k", i], scale)
                wbuf[b % (2 * PAIR), j] = w
                made[at, j] = m, total
                if j == classes - 1:
                    m, total = (jnp.concatenate([made[at, c][x] for c in range(classes)], 0) for x in range(2))
                    stat[b, 0:1, :] = to_row(m)
                    stat[b, 1:2, :] = to_row(total)
            else:
                b = pv[at]
                o = started["v", i]
                seen[at, j] = o[:ROWS, :head] + o[ROWS:, head:]
                if j == classes - 1:
                    part[b] = jnp.concatenate([seen[at, c] for c in range(classes)], 0).astype(jnp.bfloat16)

    def owner(b):
        second = b // group
        j = b - second * group
        x, y = j // (side // 2), j % (side // 2)
        spread = x * side + 2 * y + x % 2
        return j + second * (spread - j)

    def send_owned(b):
        to = owner(b)

        @pl.when(to != me)
        def _():
            push(stat.at[b], rstat.at[b // group, me], to, sent_stat.at[0], r_stat.at[b // group])
            push(part.at[b], racc.at[b // group, me], to, sent_acc.at[0], r_acc.at[b // group])

    def put_together(g, b):
        wait(rstat.at[g, pl.ds(0, group - 1)], r_stat.at[g])
        wait(racc.at[g, pl.ds(0, group - 1)], r_acc.at[g])
        racc[g, me], rstat[g, me] = part[b], stat[b]
        out[b] = joined([racc[g, c] for c in range(group)], [rstat[g, c] for c in range(group)], True)[0]

        @pl.loop(1, group)
        def _(d):
            push(out.at[b], out.at[b], device(d // side, d % side), g_sent.at[g], g_in.at[b])

    in_second = (across + along) % 2 == 0
    mine = [me, group + across * (side // 2) + along // 2]

    def send_x(b, count):
        at = pl.ds(b - square, count)
        for d in (2, 1, 3):
            to = device(0, d)
            push(stat.at[pl.ds(b, count)], xstat.at[d, at], to, sent_stat.at[1], x_stat.at[b - square])
            push(part.at[pl.ds(b, count)], xacc.at[d, at], to, sent_acc.at[1], x_acc.at[b - square])

    def by_source(here):
        return [(here - c + side) % side for c in range(side)]

    def next_y(b, count):
        i = b - square
        at = pl.ds(i, count)
        wait(xstat.at[pl.ds(1, side - 1), at], x_stat.at[i])
        wait(xacc.at[pl.ds(1, side - 1), at], x_acc.at[i])
        for k in range(i, i + count):
            xacc[0, k], xstat[0, k] = part[k + square], stat[k + square]
            slots = by_source(along)
            ypart[k], m, total = joined([xacc[s, k] for s in slots], [xstat[s, k] for s in slots], False)
            ysent[k, 0:1, :], ysent[k, 1:2, :] = m, total
        for d in (2, 1, 3):
            to = device(d, 0)
            push(ysent.at[at], ystat.at[d, at], to, sent_stat.at[2], y_stat.at[i])
            push(ypart.at[at], yacc.at[d, at], to, sent_acc.at[2], y_acc.at[i])

    def put(b, count):
        pltpu.make_async_copy(out.at[pl.ds(b, count)], o_hbm.at[pl.ds(b, count)], osem).start()

    def end_y(b, count):
        i = b - square
        at = pl.ds(i, count)
        wait(ystat.at[pl.ds(1, side - 1), at], y_stat.at[i])
        wait(yacc.at[pl.ds(1, side - 1), at], y_acc.at[i])
        for k in range(i, i + count):
            yacc[0, k], ystat[0, k] = ypart[k], ysent[k]
            slots = by_source(across)
            out[k + square] = joined([yacc[s, k] for s in slots], [ystat[s, k] for s in slots], True)[0]
        put(b, count)

    def send_straight(b):
        for dx, dy in others:
            push(part.at[b], eacc.at[b - straight, dx * side + dy], device(dx, dy), sent_acc.at[3], e_acc.at[b - straight])

    def send_straight_stat():
        for dx, dy in others:
            push(stat.at[pl.ds(straight, 2)], estat.at[dx * side + dy], device(dx, dy), sent_stat.at[3], e_stat)

    from_all = [((across - x + side) % side) * side + (along - y + side) % side for x in range(side) for y in range(side)]

    def straight_shares():
        wait(estat.at[pl.ds(1, group - 1)], e_stat)
        for i in range(2):
            estat[0, i] = stat[straight + i]
            w, _, _ = shares([estat[s, i, 0:1, :] for s in from_all], [estat[s, i, 1:2, :] for s in from_all], True)
            for c, x in enumerate(w):
                ewide[i, c] = to_column(x)

    def end_straight(b):
        i = b - straight
        wait(eacc.at[i, pl.ds(1, group - 1)], e_acc.at[i])
        eacc[i, 0] = part[b]
        seen = [ewide[i, c] * eacc[i, s].astype(jnp.float32) for c, s in enumerate(from_all)]
        out[b] = functools.reduce(jnp.add, seen).astype(jnp.bfloat16)
        put(b, 1)

    def step(first, pv=True):
        old = first - PAIR
        for i in range(PAIR):
            wait_k(first + i)
            if pv:
                wait_v(old + i)
        work([first + i for i in range(PAIR)], [old + i for i in range(PAIR)] if pv else [], lambda: None)
        more = first + slots - PAIR
        if not pv:
            load_v(more)
            load_k(more + 1)
            load_v(more + 1)
            load_k(more + 2)
            return

        @pl.when(more < n)
        def _():
            load_v(more)
            load_k(more + 1)
            load_v(more + 1)

        @pl.when(more + 2 < n)
        def _():
            load_k(more + 2)

        @pl.when(old < square)
        def _():
            for i in range(PAIR):
                send_owned(old + i)

        @pl.when(old == group + LAG - PAIR)
        def _():
            put_together(0, mine[0])

    for copy in queries:
        copy.wait()

    step(0, pv=False)

    ahead = straight - 2

    @pl.loop(PAIR, ahead, step=PAIR)
    def _(b):
        step(b)

    send_x(ahead - 4, 2)
    wait_k(ahead)
    wait_v(ahead - 2)
    wait_v(ahead - 1)
    work([ahead], [ahead - 2, ahead - 1], lambda: None)
    send_x(ahead - 2, 2)
    for b in range(ahead + 1, n):
        wait_k(b)
        wait_v(b - 1)
        work([b], [b - 1], lambda: None)
        if b == straight:
            send_x(ahead, 2)
        if b > straight:
            send_straight(b - 1)
    wait_v(n - 1)
    work([], [n - 1], lambda: None)
    send_straight(n - 1)
    send_straight_stat()

    @pl.when(in_second)
    def _():
        put_together(1, mine[1])

    for b in range(square, straight, 2):
        next_y(b, 2)
    straight_shares()
    for b in range(square, straight, 2):
        end_y(b, 2)

    @pl.loop(0, square)
    def _(b):
        @pl.when(owner(b) != me)
        def _():
            wait(out.at[b], g_in.at[b])

    put(0, square)
    for b in range(straight, n):
        end_straight(b)

    wait(out, osem)

    @pl.when(in_second)
    def _():
        wait(part.at[pl.ds(0, square - 2)], sent_acc.at[0])
        wait(stat.at[pl.ds(0, square - 2)], sent_stat.at[0])
        wait(out.at[pl.ds(0, group - 1)], g_sent.at[1])

    @pl.when(jnp.logical_not(in_second))
    def _():
        wait(part.at[pl.ds(0, square - 1)], sent_acc.at[0])
        wait(stat.at[pl.ds(0, square - 1)], sent_stat.at[0])

    wait(out.at[pl.ds(0, group - 1)], g_sent.at[0])
    for i, (acc, st) in enumerate(((xacc, xstat), (yacc, ystat)), 1):
        wait(acc.at[pl.ds(1, side - 1)], sent_acc.at[i])
        wait(st.at[pl.ds(1, side - 1)], sent_stat.at[i])
    wait(eacc.at[:, pl.ds(1, group - 1)], sent_acc.at[3])
    wait(estat.at[pl.ds(1, group - 1)], sent_stat.at[3])


def solution(mesh):
    side = math.isqrt(mesh.shape["sp"])

    def step(q, k, v):
        n, heads, head = q.shape
        tokens = k.shape[1]
        scale = head**-0.5 * math.log2(math.e)
        q, k, v = (x.reshape(x.shape[:-2] + (heads // ROWS, ROWS, head)) for x in (q, k, v))
        held = (SLOTS, tokens, heads // ROWS, ROWS, head)
        any_ = pl.BlockSpec(memory_space=pl.ANY)
        dma = pltpu.SemaphoreType.DMA
        bf16, f32 = (lambda *shape, t=t: pltpu.VMEM(shape, t) for t in (jnp.bfloat16, jnp.float32))
        group = side * side
        turns = n - 2 - group - group // 2
        return pl.pallas_call(
            functools.partial(kernel, side, scale),
            out_shape=jax.ShapeDtypeStruct((n, heads, head), q.dtype),
            in_specs=[any_] * 3,
            out_specs=any_,
            scratch_shapes=[
                pltpu.VMEM((n, heads // ROWS, 2 * ROWS, 2 * head), q.dtype),
                pltpu.VMEM(held, k.dtype),
                pltpu.VMEM(held, v.dtype),
                pltpu.VMEM((2 * PAIR, heads // ROWS, 2 * ROWS, TILES * WIDE), jnp.bfloat16),
                bf16(n, heads, head),
                f32(n, 2, 128),
                bf16(n, heads, head),
                bf16(2, group, heads, head),
                f32(2, group, 2, 128),
                bf16(side, turns, heads, head),
                f32(side, turns, 2, 128),
                bf16(turns, heads, head),
                f32(turns, 2, 128),
                bf16(side, turns, heads, head),
                f32(side, turns, 2, 128),
                bf16(2, group, heads, head),
                f32(group, 2, 2, 128),
                f32(2, group, heads, 128),
                dma((SLOTS,)),
                dma((SLOTS,)),
                dma((2,)),
                dma,
                dma((4,)),
                dma((4,)),
                dma((2,)),
                dma((2,)),
                dma((2,)),
                dma((n - 2 - turns,)),
                dma((turns,)),
                dma((turns,)),
                dma((turns,)),
                dma((turns,)),
                dma((2,)),
                dma,
            ],
            compiler_params=pltpu.CompilerParams(
                collective_id=0, has_side_effects=True, vmem_limit_bytes=60 * 2**20
            ),
            name="decode_attention",
        )(q, k, v)

    return jax.shard_map(
        step,
        mesh=mesh,
        in_specs=(P("dp", None, None), P("dp", "sp", None, None), P("dp", "sp", None, None)),
        out_specs=P("dp", None, None),
        check_vma=False,
    )
```

time: 295 us -> 56.9 us (0.19)
  waiting for transfers between devices: 198 us -> 0 us
  matrix products: 60.9 us -> 0 us
  Pallas kernels: 0 us -> 54.9 us
  other arithmetic: 18.9 us -> 0 us
  between operations: 13.4 us -> 0.01 us
    all_gather x1 -> x0, waiting for transfers between devices: 198 us -> none  [step(): return together(lax.all_gather(part_of(q, k, v), 'sp')).reshape(q.shape)]
    dot_general x2 -> x0, matrix products: 60.9 us -> none  [einsum(): return jnp.einsum(form, a.astype(jnp.float32), b.astype(jnp.float32))]
    pallas_call x0 -> x1, Pallas kernels: none -> 54.9 us  [step(): pl.pallas_call(functools.partial(kernel, side, scale), out_shape=jax.Shap...]
    reduce_sum x2 -> x0, other arithmetic: 15.2 us -> none  [the longest x1 14.1 us: together(): jnp.sum(seen * scale, 0) / jnp.sum(total * scale, 0)]
  transfers between devices with their start and end apart: 1 -> 0, of which waited for: 1 -> 0; matrix products, arithmetic and copies ran while one was open for 0% -> 0% of each run, Pallas kernels for 0% -> 0%
where the time goes in v2:
time: 56.9 us; the launch traced here: 56.7 us
  Pallas kernels  54.9 us (96%)
  local copies, waits for them, and re-layouts  1.82 us (3%)
    pallas_call x1, Pallas kernels, step(): pl.pallas_call(functools.partial(kernel, side, scale), out_shape=jax.Shap...  54.9 us
    unnamed x1, local copies, waits for them, and re-layouts  1.82 us

profile of v2, /device:TPU:97, one launch (start us, length us, event | category | flops | bytes accessed | tf_op | source)
XLA Modules:
  0.0 56.7 jit_solution(1594447571893882585)
XLA Ops:
  0.0 54.9 %decode_attention.1 = bf16[32,56,128]{2,1,0:T(8,128)(2,1)} custom-call(bf16[32,7,8,128]{3,2,1,0:T(8,128)(2,1)} %bitcast.5, bf16[32,128,7,8,128]{4,3,2,1,0:T(8,128)(2,1)} %bitcast.3, bf16[32,128,7,8,128]{4,3,2,1,0:T(8,128)(2,1)} %bitcast.4), custom_call_target="tpu_custom_call" | custom-call | tf_op jit(solution)/shard_map/decode_attention/pallas_call | solution.py:399
  54.9 1.8 %copy.5 = bf16[32,56,128]{2,1,0:T(8,128)(2,1)} copy(bf16[32,56,128]{2,1,0:T(8,128)(2,1)} %decode_attention.1) | data formatting | bytes 917504

commit v3 on v2

--- a/solution.py
+++ b/solution.py
@@ -10,7 +10,9 @@
 
 MESH = pl.DeviceIdType.MESH
 ROWS = 8
-SLOTS = 6
+SLOTS = 8
+AHEAD = 4
+STRAIGHT = 0
 PAIR = 2
 LAG = 6
 TILES = 2
@@ -69,8 +71,8 @@
 
 
 def kernel(
-    side, scale, q_hbm, k_hbm, v_hbm, o_hbm, q2, kbuf, vbuf, wbuf, part, stat, out, racc, rstat, xacc, xstat, ypart, ysent, yacc,
-    ystat, eacc, estat, ewide, ksem, vsem, qsem, osem, sent_acc, sent_stat, r_acc, r_stat, g_sent, g_in, x_acc, x_stat, y_acc,
+    side, scale, q_hbm, k_hbm, v_hbm, out, q2, kbuf, vbuf, wbuf, part, stat, racc, rstat, xacc, xstat, ypart, ysent, yacc,
+    ystat, eacc, estat, ewide, ksem, vsem, qsem, sent_acc, sent_stat, r_acc, r_stat, g_sent, g_in, x_acc, x_stat, y_acc,
     y_stat, e_acc, e_stat,
 ):
     n, classes, _, head = q_hbm.shape
@@ -79,8 +81,15 @@
     me = lax.axis_index("sp")
     across, along = me // side, me % side
 
+    group = side * side
+    square = group + group // 2
+
+    def sequence(turn):
+        turned = jnp.where(turn < group, (turn + me) % group, group + (turn + me) % (group // 2))
+        return jnp.where(turn < square, turned, turn)
+
     def load(hbm, buf, sem, b):
-        pltpu.make_async_copy(hbm.at[b], buf.at[b % slots], sem.at[b % slots]).start()
+        pltpu.make_async_copy(hbm.at[sequence(b)], buf.at[b % slots], sem.at[b % slots]).start()
 
     def loaded(buf, sem, b):
         part = buf.at[b % slots]
@@ -95,10 +104,10 @@
     ]
     for copy in queries:
         copy.start()
-    for b in range(slots - 1):
+    for b in range(slots):
+        if b >= AHEAD:
+            load_v(b - AHEAD)
         load_k(b)
-        if b < slots - PAIR:
-            load_v(b)
     zero = jnp.zeros((classes, ROWS, head), q2.dtype)
 
     @pl.loop(0, n)
@@ -106,9 +115,7 @@
         q2[b, :, :ROWS, head:] = zero
         q2[b, :, ROWS:, :head] = zero
 
-    group = side * side
-    square = group + group // 2
-    straight = n - 2
+    straight = n - STRAIGHT
 
     def device(dx, dy):
         return ((across + dx) % side) * side + (along + dy) % side
@@ -118,7 +125,6 @@
     barrier = pltpu.get_barrier_semaphore()
     for dx, dy in others:
         pl.semaphore_signal(barrier, inc=1, device_id={"sp": device(dx, dy)}, device_id_type=MESH)
-    pl.semaphore_wait(barrier, group - 1)
 
     def push(src, dst, to, send_sem, recv_sem):
         pltpu.make_async_remote_copy(
@@ -164,14 +170,14 @@
                 merge()
             elif kind == "k":
                 b = qk[at]
-                started[kind, i] = scores(q2[b, j], tile_of(kbuf, b, j))
+                started[kind, i] = scores(q2[sequence(b), j], tile_of(kbuf, b, j))
             elif kind == "v":
                 b = pv[at]
-                started[kind, i] = values_seen(wbuf[b % (2 * PAIR), j], tile_of(vbuf, b, j))
+                started[kind, i] = values_seen(wbuf[b % (2 * AHEAD), j], tile_of(vbuf, b, j))
             elif kind == "K":
                 b = qk[at]
                 w, m, total = weigh(started["k", i], scale)
-                wbuf[b % (2 * PAIR), j] = w
+                wbuf[b % (2 * AHEAD), j] = w
                 made[at, j] = m, total
                 if j == classes - 1:
                     m, total = (jnp.concatenate([made[at, c][x] for c in range(classes)], 0) for x in range(2))
@@ -192,7 +198,7 @@
         return j + second * (spread - j)
 
     def send_owned(b):
-        to = owner(b)
+        to = owner(sequence(b))
 
         @pl.when(to != me)
         def _():
@@ -200,9 +206,10 @@
             push(part.at[b], racc.at[b // group, me], to, sent_acc.at[0], r_acc.at[b // group])
 
     def put_together(g, b):
+        turn = g * group + (b - me) % (group // (g + 1))
         wait(rstat.at[g, pl.ds(0, group - 1)], r_stat.at[g])
         wait(racc.at[g, pl.ds(0, group - 1)], r_acc.at[g])
-        racc[g, me], rstat[g, me] = part[b], stat[b]
+        racc[g, me], rstat[g, me] = part[turn], stat[turn]
         out[b] = joined([racc[g, c] for c in range(group)], [rstat[g, c] for c in range(group)], True)[0]
 
         @pl.loop(1, group)
@@ -237,9 +244,6 @@
             push(ysent.at[at], ystat.at[d, at], to, sent_stat.at[2], y_stat.at[i])
             push(ypart.at[at], yacc.at[d, at], to, sent_acc.at[2], y_acc.at[i])
 
-    def put(b, count):
-        pltpu.make_async_copy(out.at[pl.ds(b, count)], o_hbm.at[pl.ds(b, count)], osem).start()
-
     def end_y(b, count):
         i = b - square
         at = pl.ds(i, count)
@@ -249,7 +253,6 @@
             yacc[0, k], ystat[0, k] = ypart[k], ysent[k]
             slots = by_source(across)
             out[k + square] = joined([yacc[s, k] for s in slots], [ystat[s, k] for s in slots], True)[0]
-        put(b, count)
 
     def send_straight(b):
         for dx, dy in others:
@@ -257,13 +260,13 @@
 
     def send_straight_stat():
         for dx, dy in others:
-            push(stat.at[pl.ds(straight, 2)], estat.at[dx * side + dy], device(dx, dy), sent_stat.at[3], e_stat)
+            push(stat.at[pl.ds(straight, STRAIGHT)], estat.at[dx * side + dy], device(dx, dy), sent_stat.at[3], e_stat)
 
     from_all = [((across - x + side) % side) * side + (along - y + side) % side for x in range(side) for y in range(side)]
 
     def straight_shares():
         wait(estat.at[pl.ds(1, group - 1)], e_stat)
-        for i in range(2):
+        for i in range(STRAIGHT):
             estat[0, i] = stat[straight + i]
             w, _, _ = shares([estat[s, i, 0:1, :] for s in from_all], [estat[s, i, 1:2, :] for s in from_all], True)
             for c, x in enumerate(w):
@@ -275,32 +278,31 @@
         eacc[i, 0] = part[b]
         seen = [ewide[i, c] * eacc[i, s].astype(jnp.float32) for c, s in enumerate(from_all)]
         out[b] = functools.reduce(jnp.add, seen).astype(jnp.bfloat16)
-        put(b, 1)
 
     def step(first, pv=True):
-        old = first - PAIR
+        old = first - AHEAD
         for i in range(PAIR):
             wait_k(first + i)
             if pv:
                 wait_v(old + i)
         work([first + i for i in range(PAIR)], [old + i for i in range(PAIR)] if pv else [], lambda: None)
-        more = first + slots - PAIR
+
+        def more(i):
+            load_v(old + slots + i)
+
+            @pl.when(first + slots + i < n)
+            def _():
+                load_k(first + slots + i)
+
         if not pv:
-            load_v(more)
-            load_k(more + 1)
-            load_v(more + 1)
-            load_k(more + 2)
+            for i in range(PAIR):
+                more(i)
             return
 
-        @pl.when(more < n)
+        @pl.when(old + slots < n)
         def _():
-            load_v(more)
-            load_k(more + 1)
-            load_v(more + 1)
-
-        @pl.when(more + 2 < n)
-        def _():
-            load_k(more + 2)
+            for i in range(PAIR):
+                more(i)
 
         @pl.when(old < square)
         def _():
@@ -314,42 +316,41 @@
     for copy in queries:
         copy.wait()
 
-    step(0, pv=False)
-
-    ahead = straight - 2
-
-    @pl.loop(PAIR, ahead, step=PAIR)
+    @pl.loop(0, AHEAD, step=PAIR)
+    def _(b):
+        step(b, pv=False)
+
+    pl.semaphore_wait(barrier, group - 1)
+
+    @pl.loop(AHEAD, n - PAIR, step=PAIR)
     def _(b):
         step(b)
 
-    send_x(ahead - 4, 2)
-    wait_k(ahead)
-    wait_v(ahead - 2)
-    wait_v(ahead - 1)
-    work([ahead], [ahead - 2, ahead - 1], lambda: None)
-    send_x(ahead - 2, 2)
-    for b in range(ahead + 1, n):
-        wait_k(b)
-        wait_v(b - 1)
-        work([b], [b - 1], lambda: None)
-        if b == straight:
-            send_x(ahead, 2)
-        if b > straight:
-            send_straight(b - 1)
-    wait_v(n - 1)
-    work([], [n - 1], lambda: None)
-    send_straight(n - 1)
-    send_straight_stat()
+    turns = [(square, 2)]
+    send_x(*turns[-1])
+    for qk, pv in (([n - 2], [n - 6, n - 5]), ([n - 1], [n - 4]), ([], [n - 3, n - 2]), ([], [n - 1])):
+        for b in qk:
+            wait_k(b)
+        for b in pv:
+            wait_v(b)
+        work(qk, pv, lambda: None)
+        if pv[-1] < straight:
+            turns.append((pv[0], len(pv)))
+            send_x(*turns[-1])
+        else:
+            send_straight(n - 1)
+            send_straight_stat()
 
     @pl.when(in_second)
     def _():
         put_together(1, mine[1])
 
-    for b in range(square, straight, 2):
-        next_y(b, 2)
-    straight_shares()
-    for b in range(square, straight, 2):
-        end_y(b, 2)
+    for turn in turns:
+        next_y(*turn)
+    if STRAIGHT:
+        straight_shares()
+    for turn in turns[:-1]:
+        end_y(*turn)
 
     @pl.loop(0, square)
     def _(b):
@@ -357,11 +358,9 @@
         def _():
             wait(out.at[b], g_in.at[b])
 
-    put(0, square)
+    end_y(*turns[-1])
     for b in range(straight, n):
         end_straight(b)
-
-    wait(out, osem)
 
     @pl.when(in_second)
     def _():
@@ -378,8 +377,9 @@
     for i, (acc, st) in enumerate(((xacc, xstat), (yacc, ystat)), 1):
         wait(acc.at[pl.ds(1, side - 1)], sent_acc.at[i])
         wait(st.at[pl.ds(1, side - 1)], sent_stat.at[i])
-    wait(eacc.at[:, pl.ds(1, group - 1)], sent_acc.at[3])
-    wait(estat.at[pl.ds(1, group - 1)], sent_stat.at[3])
+    if STRAIGHT:
+        wait(eacc.at[:, pl.ds(1, group - 1)], sent_acc.at[3])
+        wait(estat.at[pl.ds(1, group - 1)], sent_stat.at[3])
 
 
 def solution(mesh):
@@ -395,20 +395,19 @@
         dma = pltpu.SemaphoreType.DMA
         bf16, f32 = (lambda *shape, t=t: pltpu.VMEM(shape, t) for t in (jnp.bfloat16, jnp.float32))
         group = side * side
-        turns = n - 2 - group - group // 2
-        return pl.pallas_call(
+        turns = n - STRAIGHT - group - group // 2
+        held_out = pl.pallas_call(
             functools.partial(kernel, side, scale),
-            out_shape=jax.ShapeDtypeStruct((n, heads, head), q.dtype),
-            in_specs=[any_] * 3,
-            out_specs=any_,
+            out_shape=jax.ShapeDtypeStruct((n + 1, heads, head), q.dtype),
+            in_specs=[pl.BlockSpec(memory_space=pltpu.HBM)] * 3,
+            out_specs=pl.BlockSpec(memory_space=pltpu.VMEM),
             scratch_shapes=[
                 pltpu.VMEM((n, heads // ROWS, 2 * ROWS, 2 * head), q.dtype),
                 pltpu.VMEM(held, k.dtype),
                 pltpu.VMEM(held, v.dtype),
-                pltpu.VMEM((2 * PAIR, heads // ROWS, 2 * ROWS, TILES * WIDE), jnp.bfloat16),
+                pltpu.VMEM((2 * AHEAD, heads // ROWS, 2 * ROWS, TILES * WIDE), jnp.bfloat16),
                 bf16(n, heads, head),
                 f32(n, 2, 128),
-                bf16(n, heads, head),
                 bf16(2, group, heads, head),
                 f32(2, group, 2, 128),
                 bf16(side, turns, heads, head),
@@ -417,19 +416,18 @@
                 f32(turns, 2, 128),
                 bf16(side, turns, heads, head),
                 f32(side, turns, 2, 128),
-                bf16(2, group, heads, head),
-                f32(group, 2, 2, 128),
-                f32(2, group, heads, 128),
+                bf16(max(STRAIGHT, 1), group, heads, head),
+                f32(group, max(STRAIGHT, 1), 2, 128),
+                f32(max(STRAIGHT, 1), group, heads, 128),
                 dma((SLOTS,)),
                 dma((SLOTS,)),
                 dma((2,)),
-                dma,
                 dma((4,)),
                 dma((4,)),
                 dma((2,)),
                 dma((2,)),
                 dma((2,)),
-                dma((n - 2 - turns,)),
+                dma((group + group // 2,)),
                 dma((turns,)),
                 dma((turns,)),
                 dma((turns,)),
@@ -438,10 +436,11 @@
                 dma,
             ],
             compiler_params=pltpu.CompilerParams(
-                collective_id=0, has_side_effects=True, vmem_limit_bytes=60 * 2**20
+                collective_id=0, has_side_effects=True, vmem_limit_bytes=46 * 2**20
             ),
             name="decode_attention",
-        )(q, k, v)
+        )(*(pltpu.with_memory_space_constraint(x, pltpu.HBM) for x in (q, k, v)))
+        return held_out[:n]
 
     return jax.shard_map(
         step,

time: 56.9 us -> 54.4 us (0.956)
  Pallas kernels: 54.9 us -> 53.5 us
  local copies, waits for them, and re-layouts: 1.82 us -> 0.8 us
    unnamed x1 -> x0, local copies, waits for them, and re-layouts: 1.82 us -> none
    pallas_call x1, Pallas kernels: 54.9 us -> 53.5 us  [step(): pl.pallas_call(functools.partial(kernel, side, scale), out_shape=jax.Shap...]
    slice x0 -> x1, local copies, waits for them, and re-layouts: none -> 0.8 us  [step(): return held_out[:n]]
where the time goes in v3:
time: 54.4 us; the launch traced here: 54.3 us
  Pallas kernels  53.5 us (98%)
  local copies, waits for them, and re-layouts  0.8 us (1%)
    pallas_call x1, Pallas kernels, step(): pl.pallas_call(functools.partial(kernel, side, scale), out_shape=jax.Shap...  53.5 us

profile of v3, /device:TPU:97, one launch (start us, length us, event | category | flops | bytes accessed | tf_op | source)
XLA Modules:
  0.0 54.3 jit_solution(8962308736803709714)
XLA Ops:
  0.0 53.5 %decode_attention.1 = bf16[33,56,128]{2,1,0:T(8,128)(2,1)S(1)} custom-call(bf16[32,7,8,128]{3,2,1,0:T(8,128)(2,1)} %bitcast.5, bf16[32,128,7,8,128]{4,3,2,1,0:T(8,128)(2,1)} %bitcast.3, bf16[32,128,7,8,128]{4,3,2,1,0:T(8,128)(2,1)} %bitcast.4), custom_call_target="tpu_custom_call" | custom-call | tf_op jit(solution)/shard_map/decode_attention/pallas_call | solution.py:399
  53.5 0.8 %slice.3 = bf16[32,56,128]{2,1,0:T(8,128)(2,1)} slice(bf16[33,56,128]{2,1,0:T(8,128)(2,1)S(1)} %decode_attention.1), slice={[0:32], [0:56], [0:128]} | slice | bytes 917504 | tf_op jit(solution)/shard_map/slice | solution.py:443

commit v4 on v3

--- a/solution.py
+++ b/solution.py
@@ -220,64 +220,64 @@
     mine = [me, group + across * (side // 2) + along // 2]
 
     def send_x(b, count):
-        at = pl.ds(b - square, count)
         for d in (2, 1, 3):
-            to = device(0, d)
+            to, at = device(0, d), pl.ds(b - square, count)
+            push(part.at[pl.ds(b, count)], xacc.at[d, at], to, sent_acc.at[1], x_acc.at[b - square])
+
+    def send_x_stat(b, count):
+        for d in (2, 1, 3):
+            to, at = device(0, d), pl.ds(b - square, count)
             push(stat.at[pl.ds(b, count)], xstat.at[d, at], to, sent_stat.at[1], x_stat.at[b - square])
-            push(part.at[pl.ds(b, count)], xacc.at[d, at], to, sent_acc.at[1], x_acc.at[b - square])
 
     def by_source(here):
         return [(here - c + side) % side for c in range(side)]
+
+    def summed(accs, columns):
+        seen = functools.reduce(jnp.add, [w * acc.astype(jnp.float32) for w, acc in zip(columns, accs)])
+        return seen.astype(jnp.bfloat16)
 
     def next_y(b, count):
         i = b - square
         at = pl.ds(i, count)
+        slots = by_source(along)
+        columns = []
         wait(xstat.at[pl.ds(1, side - 1), at], x_stat.at[i])
-        wait(xacc.at[pl.ds(1, side - 1), at], x_acc.at[i])
         for k in range(i, i + count):
-            xacc[0, k], xstat[0, k] = part[k + square], stat[k + square]
-            slots = by_source(along)
-            ypart[k], m, total = joined([xacc[s, k] for s in slots], [xstat[s, k] for s in slots], False)
+            xstat[0, k] = stat[k + square]
+            w, m, total = shares([xstat[s, k, 0:1, :] for s in slots], [xstat[s, k, 1:2, :] for s in slots], False)
             ysent[k, 0:1, :], ysent[k, 1:2, :] = m, total
+            columns.append([to_column(x) for x in w])
         for d in (2, 1, 3):
-            to = device(d, 0)
-            push(ysent.at[at], ystat.at[d, at], to, sent_stat.at[2], y_stat.at[i])
-            push(ypart.at[at], yacc.at[d, at], to, sent_acc.at[2], y_acc.at[i])
+            push(ysent.at[at], ystat.at[d, at], device(d, 0), sent_stat.at[2], y_stat.at[i])
+
+        def finish():
+            wait(xacc.at[pl.ds(1, side - 1), at], x_acc.at[i])
+            for k in range(i, i + count):
+                xacc[0, k] = part[k + square]
+                ypart[k] = summed([xacc[s, k] for s in slots], columns[k - i])
+            for d in (2, 1, 3):
+                push(ypart.at[at], yacc.at[d, at], device(d, 0), sent_acc.at[2], y_acc.at[i])
+
+        return finish
 
     def end_y(b, count):
         i = b - square
         at = pl.ds(i, count)
+        slots = by_source(across)
+        columns = []
         wait(ystat.at[pl.ds(1, side - 1), at], y_stat.at[i])
-        wait(yacc.at[pl.ds(1, side - 1), at], y_acc.at[i])
         for k in range(i, i + count):
-            yacc[0, k], ystat[0, k] = ypart[k], ysent[k]
-            slots = by_source(across)
-            out[k + square] = joined([yacc[s, k] for s in slots], [ystat[s, k] for s in slots], True)[0]
-
-    def send_straight(b):
-        for dx, dy in others:
-            push(part.at[b], eacc.at[b - straight, dx * side + dy], device(dx, dy), sent_acc.at[3], e_acc.at[b - straight])
-
-    def send_straight_stat():
-        for dx, dy in others:
-            push(stat.at[pl.ds(straight, STRAIGHT)], estat.at[dx * side + dy], device(dx, dy), sent_stat.at[3], e_stat)
-
-    from_all = [((across - x + side) % side) * side + (along - y + side) % side for x in range(side) for y in range(side)]
-
-    def straight_shares():
-        wait(estat.at[pl.ds(1, group - 1)], e_stat)
-        for i in range(STRAIGHT):
-            estat[0, i] = stat[straight + i]
-            w, _, _ = shares([estat[s, i, 0:1, :] for s in from_all], [estat[s, i, 1:2, :] for s in from_all], True)
-            for c, x in enumerate(w):
-                ewide[i, c] = to_column(x)
-
-    def end_straight(b):
-        i = b - straight
-        wait(eacc.at[i, pl.ds(1, group - 1)], e_acc.at[i])
-        eacc[i, 0] = part[b]
-        seen = [ewide[i, c] * eacc[i, s].astype(jnp.float32) for c, s in enumerate(from_all)]
-        out[b] = functools.reduce(jnp.add, seen).astype(jnp.bfloat16)
+            ystat[0, k] = ysent[k]
+            w, _, _ = shares([ystat[s, k, 0:1, :] for s in slots], [ystat[s, k, 1:2, :] for s in slots], True)
+            columns.append([to_column(x) for x in w])
+
+        def finish():
+            wait(yacc.at[pl.ds(1, side - 1), at], y_acc.at[i])
+            for k in range(i, i + count):
+                yacc[0, k] = ypart[k]
+                out[k + square] = summed([yacc[s, k] for s in slots], columns[k - i])
+
+        return finish
 
     def step(first, pv=True):
         old = first - AHEAD
@@ -326,31 +326,33 @@
     def _(b):
         step(b)
 
-    turns = [(square, 2)]
-    send_x(*turns[-1])
-    for qk, pv in (([n - 2], [n - 6, n - 5]), ([n - 1], [n - 4]), ([], [n - 3, n - 2]), ([], [n - 1])):
+    turns = [(square, 2), (square + 2, 2), (square + 4, 1), (square + 5, 2), (square + 7, 1)]
+    for turn in turns[:3]:
+        send_x_stat(*turn)
+    send_x(*turns[0])
+    for qk, turn in zip(([n - 2], [n - 1], [], []), turns[1:]):
+        pv = [turn[0] + i for i in range(turn[1])]
         for b in qk:
             wait_k(b)
         for b in pv:
             wait_v(b)
         work(qk, pv, lambda: None)
-        if pv[-1] < straight:
-            turns.append((pv[0], len(pv)))
-            send_x(*turns[-1])
-        else:
-            send_straight(n - 1)
-            send_straight_stat()
+        send_x(*turn)
+        if qk:
+            send_x_stat(*turns[3 + qk[0] - (n - 2)])
 
     @pl.when(in_second)
     def _():
         put_together(1, mine[1])
 
-    for turn in turns:
-        next_y(*turn)
-    if STRAIGHT:
-        straight_shares()
-    for turn in turns[:-1]:
-        end_y(*turn)
+    def in_turn(act):
+        for turn in turns[:3]:
+            act(*turn)()
+        return [act(*turn) for turn in turns[3:]]
+
+    for finish in in_turn(next_y):
+        finish()
+    last = in_turn(end_y)
 
     @pl.loop(0, square)
     def _(b):
@@ -358,9 +360,8 @@
         def _():
             wait(out.at[b], g_in.at[b])
 
-    end_y(*turns[-1])
-    for b in range(straight, n):
-        end_straight(b)
+    for finish in last:
+        finish()
 
     @pl.when(in_second)
     def _():
@@ -377,9 +378,6 @@
     for i, (acc, st) in enumerate(((xacc, xstat), (yacc, ystat)), 1):
         wait(acc.at[pl.ds(1, side - 1)], sent_acc.at[i])
         wait(st.at[pl.ds(1, side - 1)], sent_stat.at[i])
-    if STRAIGHT:
-        wait(eacc.at[:, pl.ds(1, group - 1)], sent_acc.at[3])
-        wait(estat.at[pl.ds(1, group - 1)], sent_stat.at[3])
 
 
 def solution(mesh):

time: 54.4 us -> 53.7 us (0.987)
  Pallas kernels: 53.5 us -> 52.9 us
    pallas_call x1, Pallas kernels: 53.5 us -> 52.9 us  [step(): pl.pallas_call(functools.partial(kernel, side, scale), out_shape=jax.Shap...]
where the time goes in v4:
time: 53.7 us
  Pallas kernels  52.9 us (99%)
  local copies, waits for them, and re-layouts  0.8 us (1%)
    pallas_call x1, Pallas kernels, step(): pl.pallas_call(functools.partial(kernel, side, scale), out_shape=jax.Shap...  52.9 us

profile of v4, /device:TPU:97, one launch (start us, length us, event | category | flops | bytes accessed | tf_op | source)
XLA Modules:
  0.0 53.7 jit_solution(8613903286105909302)
XLA Ops:
  0.0 52.9 %decode_attention.1 = bf16[33,56,128]{2,1,0:T(8,128)(2,1)S(1)} custom-call(bf16[32,7,8,128]{3,2,1,0:T(8,128)(2,1)} %bitcast.5, bf16[32,128,7,8,128]{4,3,2,1,0:T(8,128)(2,1)} %bitcast.3, bf16[32,128,7,8,128]{4,3,2,1,0:T(8,128)(2,1)} %bitcast.4), custom_call_target="tpu_custom_call" | custom-call | tf_op jit(solution)/shard_map/decode_attention/pallas_call | solution.py:397
  52.9 0.8 %slice.3 = bf16[32,56,128]{2,1,0:T(8,128)(2,1)} slice(bf16[33,56,128]{2,1,0:T(8,128)(2,1)S(1)} %decode_attention.1), slice={[0:32], [0:56], [0:128]} | slice | bytes 917504 | tf_op jit(solution)/shard_map/slice | solution.py:441
